TPU v7x, 32 devices: a whole 2x2x4 slice. The times are simulated.
32 devices in a mesh: seq: 8 (over z, y), batch: 4 (over x, core).
Axes of the slice: x: 2, y: 2, z: 4, core: 2. Of those that a mesh axis runs over, the one named last changes fastest.
Arguments:
- queries: bfloat16 [4, 4096, 16, 128], P('batch', 'seq'), may hold values from -5 to 5
- keys: bfloat16 [4, 4096, 16, 128], P('batch', 'seq'), may hold values from -5 to 5
- values: bfloat16 [4, 4096, 16, 128], P('batch', 'seq'), may hold values from -5 to 5
- keep_count: int32 [4, 16, 32], P('batch'), may hold values from 0 to 128
- query_map: bfloat16 [16, 128, 8], replicated, may hold values from -0.5 to 0.5
- key_map: bfloat16 [16, 128, 8], replicated, may hold values from -0.5 to 0.5
- cotangent: bfloat16 [4, 4096, 16, 128], P('batch', 'seq'), may hold values from -5 to 5
Outputs:
- attended: bfloat16 [4, 4096, 16, 128], P('batch', 'seq')
- grad_query_map: float32 [16, 128, 8], replicated
- grad_key_map: float32 [16, 128, 8], replicated
All inputs are finite; a program needn't handle non-finite values.
Results may differ from a plain program's by a relative error of at most 0.0035.
Values may be sent and summed in bfloat16 or wider, within the bound.
A program may use at most 128 MiB of HBM per device.

v0:
```python
import math
import jax
import jax.numpy as jnp
from jax import lax
from jax.sharding import PartitionSpec as P

TILE = 128
WINDOW = 256
HIGHEST = lax.Precision.HIGHEST
feature_shift = 1.5


def passed_along(value, axis, steps):
    count = lax.axis_size(axis)
    first, last = (max(0, -steps), min(count, count - steps))
    return lax.ppermute(value, axis, [(source, source + steps) for source in range(first, last)])


def prefix(shard, axis, combine, identity, reverse):
    peers, position = (lax.axis_size(axis), lax.axis_index(axis))
    everything = jax.tree.map(lambda part: lax.all_gather(part, axis), shard)
    start = jax.tree.map(
        lambda part, zero: jnp.broadcast_to(jnp.asarray(zero, part.dtype), part.shape),
        shard,
        identity,
    )

    def step(k, before):
        at = peers - 1 - k if reverse else k
        reached = at > position if reverse else at < position
        new = combine(before, jax.tree.map(lambda part: part[at], everything))
        return jax.tree.map(lambda a, b: jnp.where(reached, a, b), new, before)

    return lax.fori_loop(0, peers, step, start)


def add_pair(earlier, later):
    return (earlier[0] + later[0], earlier[1] + later[1])


def windowed(tiled, first, count, span):
    pieces = [
        lax.slice_in_dim(tiled, first + offset, first + offset + count, axis=0)
        for offset in range(span)
    ]
    return jnp.concatenate(pieces, 1)


def body(queries, keys, values, keep_count, query_map, key_map, cotangent):
    q_rows = queries[0]
    k_rows = keys[0]
    v_rows = values[0]
    cot_rows = cotangent[0].astype(jnp.float32)
    tokens, heads, width = q_rows.shape
    rank = query_map.shape[2]
    tiles_dev = tokens // TILE
    span = WINDOW // TILE
    scale = 1.0 / math.sqrt(width)
    index = lax.axis_index("seq")
    halo_rows = WINDOW - TILE
    prev_keys, prev_values = passed_along(
        (k_rows[tokens - halo_rows :], v_rows[tokens - halo_rows :]), "seq", 1
    )
    halo_tiles = halo_rows // TILE
    ext_tiles = halo_tiles + tiles_dev
    ext_rows = halo_rows + tokens
    ext_keys = jnp.concatenate([prev_keys, k_rows], 0)
    ext_values = jnp.concatenate([prev_values, v_rows], 0)
    counts = keep_count[0]
    padded_counts = jnp.concatenate([jnp.zeros((heads, tiles_dev), jnp.int32), counts], 1)
    count_start = index * tiles_dev + tiles_dev - halo_tiles
    ext_counts = lax.dynamic_slice_in_dim(padded_counts, count_start, ext_tiles, 1)
    local = jnp.arange(ext_rows, dtype=jnp.int32)
    key_pos = index * tokens - halo_rows + local
    valid = key_pos >= 0
    within = local % TILE
    kept = within[None, :] < jnp.repeat(ext_counts, TILE, axis=1)
    evicted = valid[None, :] & jnp.logical_not(kept)
    pre_q = (
        jnp.einsum("thd,hdr->thr", q_rows, query_map, preferred_element_type=jnp.float32)
        - feature_shift
    )
    pre_k = (
        jnp.einsum("thd,hdr->thr", ext_keys, key_map, preferred_element_type=jnp.float32)
        - feature_shift
    )
    feat_q = jax.nn.softplus(pre_q)
    feat_k = jax.nn.softplus(pre_k)
    valid_f = valid.astype(jnp.float32)[:, None, None]
    evict_f = evicted.T.astype(jnp.float32)[:, :, None]
    v_tiles = ext_values.astype(jnp.float32).reshape(ext_tiles, TILE, heads, width)

    def tile_state(feat):
        tiled = feat.reshape(ext_tiles, TILE, heads, rank)
        return (jnp.einsum("nthr,nthd->nhrd", tiled, v_tiles, precision=HIGHEST), jnp.sum(tiled, 1))

    all_state, all_norm = tile_state(feat_k * valid_f)
    ev_state, ev_norm = tile_state(feat_k * evict_f)
    q_tile = jnp.arange(tiles_dev, dtype=jnp.int32)[:, None] + halo_tiles
    k_tile = jnp.arange(ext_tiles, dtype=jnp.int32)[None, :]
    in_halo = (k_tile < halo_tiles).astype(jnp.float32)
    far_mix = (k_tile < q_tile - span + 1).astype(jnp.float32)
    near_mix = ((k_tile >= q_tile - span + 1) & (k_tile < q_tile)).astype(jnp.float32)
    far_coef = far_mix * (1.0 - in_halo) - near_mix * in_halo
    carried_state = jnp.sum(all_state[halo_tiles:], 0)
    carried_norm = jnp.sum(all_norm[halo_tiles:], 0)
    far_state, far_norm = prefix(
        (carried_state, carried_norm),
        "seq",
        add_pair,
        (jnp.zeros_like(carried_state), jnp.zeros_like(carried_norm)),
        False,
    )
    state = (
        far_state[None]
        + jnp.einsum("jn,nhrd->jhrd", far_coef, all_state, precision=HIGHEST)
        + jnp.einsum("jn,nhrd->jhrd", near_mix, ev_state, precision=HIGHEST)
    )
    norm = (
        far_norm[None]
        + jnp.einsum("jn,nhr->jhr", far_coef, all_norm, precision=HIGHEST)
        + jnp.einsum("jn,nhr->jhr", near_mix, ev_norm, precision=HIGHEST)
    )
    first_tile = halo_tiles - span + 1
    key_window = windowed(
        ext_keys.reshape(ext_tiles, TILE, heads, width), first_tile, tiles_dev, span
    )
    value_window = windowed(
        ext_values.reshape(ext_tiles, TILE, heads, width), first_tile, tiles_dev, span
    )
    allowed = (kept & valid[None, :]).T.reshape(ext_tiles, TILE, heads)
    allowed_window = windowed(allowed, first_tile, tiles_dev, span).transpose(0, 2, 1)
    slot = jnp.arange(span * TILE, dtype=jnp.int32)
    own_slot = slot >= (span - 1) * TILE
    causal = slot[None, :] - (span - 1) * TILE <= jnp.arange(TILE, dtype=jnp.int32)[:, None]
    live_pairs = jnp.where(
        own_slot[None, None, None, :], causal[None, None], allowed_window[:, :, None, :]
    )
    q_tiles = q_rows.reshape(tiles_dev, TILE, heads, width)
    scores = (
        jnp.einsum("nqhd,nkhd->nhqk", q_tiles, key_window, preferred_element_type=jnp.float32)
        * scale
    )
    row_max = jnp.max(jnp.where(live_pairs, scores, -jnp.inf), -1)
    weights = jnp.where(live_pairs, jnp.exp(scores - row_max[..., None]), 0.0)
    denom = jnp.sum(weights, -1).transpose(0, 2, 1).reshape(tokens, heads)
    numer = jnp.einsum(
        "nhqk,nkhd->nqhd",
        weights.astype(jnp.bfloat16),
        value_window,
        preferred_element_type=jnp.float32,
    ).reshape(tokens, heads, width)
    decay = jnp.exp(-row_max.transpose(0, 2, 1).reshape(tokens, heads))
    feat_qt = feat_q.reshape(tiles_dev, TILE, heads, rank)
    kernel_num = jnp.einsum("nthr,nhrd->nthd", feat_qt, state, precision=HIGHEST).reshape(
        tokens, heads, width
    )
    kernel_den = jnp.einsum("nthr,nhr->nth", feat_qt, norm, precision=HIGHEST).reshape(
        tokens, heads
    )
    total = denom + decay * kernel_den
    out = (numer + decay[..., None] * kernel_num) / total[..., None]
    delta = cot_rows / total[..., None]
    ratio_grad = -jnp.sum(delta * out, -1)
    grad_num = (decay[..., None] * delta).reshape(tiles_dev, TILE, heads, width)
    grad_den = (decay * ratio_grad).reshape(tiles_dev, TILE, heads)
    grad_fq = (
        jnp.einsum("nthd,nhrd->nthr", grad_num, state, precision=HIGHEST)
        + grad_den[..., None] * norm[:, None]
    )
    d_state = jnp.einsum("nthr,nthd->nhrd", feat_qt, grad_num, precision=HIGHEST)
    d_norm = jnp.einsum("nthr,nth->nhr", feat_qt, grad_den, precision=HIGHEST)
    own_state = jnp.sum(d_state, 0)
    own_norm = jnp.sum(d_norm, 0)
    after_state, after_norm = prefix(
        (own_state, own_norm),
        "seq",
        add_pair,
        (jnp.zeros_like(own_state), jnp.zeros_like(own_norm)),
        True,
    )
    own_tiles = (jnp.arange(ext_tiles, dtype=jnp.int32) >= halo_tiles).astype(jnp.float32)
    d_all = (
        jnp.einsum("jn,jhrd->nhrd", far_coef, d_state, precision=HIGHEST)
        + own_tiles[:, None, None, None] * after_state[None]
    )
    d_alln = (
        jnp.einsum("jn,jhr->nhr", far_coef, d_norm, precision=HIGHEST)
        + own_tiles[:, None, None] * after_norm[None]
    )
    d_ev = jnp.einsum("jn,jhrd->nhrd", near_mix, d_state, precision=HIGHEST)
    d_evn = jnp.einsum("jn,jhr->nhr", near_mix, d_norm, precision=HIGHEST)
    grad_all = jnp.einsum("nhrd,nthd->nthr", d_all, v_tiles, precision=HIGHEST) + d_alln[:, None]
    grad_ev = jnp.einsum("nhrd,nthd->nthr", d_ev, v_tiles, precision=HIGHEST) + d_evn[:, None]
    grad_fk = valid_f * grad_all.reshape(ext_rows, heads, rank) + evict_f * grad_ev.reshape(
        ext_rows, heads, rank
    )
    grad_pre_k = grad_fk * jax.nn.sigmoid(pre_k)
    grad_pre_q = grad_fq.reshape(tokens, heads, rank) * jax.nn.sigmoid(pre_q)
    grad_q = jnp.einsum("thd,thr->hdr", q_rows.astype(jnp.float32), grad_pre_q, precision=HIGHEST)
    grad_k = jnp.einsum("thd,thr->hdr", ext_keys.astype(jnp.float32), grad_pre_k, precision=HIGHEST)
    grad_q, grad_k = lax.psum((grad_q, grad_k), ("seq", "batch"))
    return (out.astype(jnp.bfloat16)[None], grad_q, grad_k)


def solution(mesh):
    placed = (
        P("batch", "seq", None, None),
        P("batch", "seq", None, None),
        P("batch", "seq", None, None),
        P("batch", None, None),
        P(),
        P(),
        P("batch", "seq", None, None),
    )
    return jax.shard_map(
        body,
        mesh=mesh,
        in_specs=placed,
        out_specs=(P("batch", "seq", None, None), P(), P()),
        check_vma=False,
    )
```

profile of v0, /device:TPU:0, one launch (start us, length us, event | category | flops | bytes accessed | tf_op | source)
XLA Modules:
  0.0 420.2 jit_solution(9056168187303462686)
XLA Ops:
  11.7 5.7 %collective-permute-start.1 = (bf16[128,16,128]{2,0,1:T(8,128)(2,1)}, bf16[128,16,128]{2,0,1:T(8,128)(2,1)}, u32[]{:S(2)}, u32[]{:S(2)}) collective-permute-start(bf16[128,16,128]{2,0,1:T(8,128)(2,1)} %slice_bitcast_fusion), channel_id=1, source_target_pairs={{0,4},{4,8},{8,12},{12,16},{16,20},{20,24},{24,28},{1,5},{5,9},{9,... | collective-permute-start | bytes 1572872 | tf_op jit(solution)/shard_map/ppermute | solution.py:16
  19.3 2.7 collective-permute-start
  26.0 3.5 copy.177
  45.3 35.2 %all-gather = f32[128,8,128]{2,1,0:T(8,128)} all-gather(f32[16,8,128]{2,1,0:T(8,128)S(1)} %slice_reduce_fusion), channel_id=2, replica_groups=mesh['seq'=8,'batch'=4] {'seq'}, dimensions={0}, use_global_device_ids=true | all-gather | bytes 589824 | tf_op jit(solution)/shard_map/all_gather | solution.py:21
  80.6 30.6 %all-gather.4 = f32[8,16,8]{1,2,0:T(8,128)S(1)} all-gather(f32[1,16,8]{1,2,0:T(8,128)S(1)} %bitcast.246), channel_id=3, replica_groups=mesh['seq'=8,'batch'=4] {'seq'}, dimensions={0}, use_global_device_ids=true | all-gather | bytes 4608 | tf_op jit(solution)/shard_map/all_gather | solution.py:21
  111.2 7.7 %while.34 = (s32[]{:T(128)}, f32[16,8,128]{2,1,0:T(8,128)S(1)}, f32[16,8]{0,1:T(8,128)S(1)}, s32[]{:T(128)}, f32[8,16,8,128]{3,2,1,0:T(8,128)}, /*index=5*/f32[8,16,8]{1,2,0:T(8,128)S(1)}, s32[]{:T(128)}, s32[]{:T(128)}) while((s32[]{:T(128)}, f32[16,8,128]{2,1,0:T(8,128)S(1)}, f32[16,8]{0,1:T(8,128)S(1)}, s32[]{:T(128)}, ...), condition=%wide.region_5.6_spmd.clone, body=%wide.region_4.5_spmd.clone.sunk | while | flops 49540 | bytes 198259 | solution.py:34
  118.9 3.9 fusion.42
  124.9 6.7 %convolution_bitcast_fusion = f32[4,128,16,128]{3,1,2,0:T(8,128)S(1)} fusion(f32[4,16,8,128]{3,0,2,1:T(4,128)S(1)} %fusion.66, f32[512,16,8]{0,2,1:T(8,128)S(1)} %copy-done.13), kind=kOutput, calls=%fused_computation.42 | convolution fusion | flops 101056512 | bytes 4718592 | tf_op jit(solution)/shard_map/nthr,nhrd->nthd/dot_general | solution.py:155
  131.6 4.5 %copy.193 = f32[4,128,16,128]{3,2,1,0:T(8,128)} copy(f32[4,128,16,128]{3,1,2,0:T(8,128)S(1)} %convolution_bitcast_fusion) | data formatting | bytes 8388608 | tf_op jit(solution)/shard_map/nthr,nhrd->nthd/transpose | solution.py:155
  139.9 2.9 fusion
  143.5 4.1 fusion.2
  152.3 6.3 %fusion.27 = f32[4,128,16,128]{3,1,2,0:T(8,128)S(1)} fusion(f32[4,16,256,128]{3,2,1,0:T(8,128)S(1)} %copy-done.10, f32[4,16,128]{2,1,0:T(8,128)S(1)} %get-tuple-element.356, pred[4,16,256]{2,1,0:T(8,128)(4,1)S(1)} %copy-done.26, pred[128,256]{0,1:T(8,128)(4,1)S(1)} %copy-done.21, pred[256]{0:T(512)(128)(4,1)S(1)} %copy-done.42, ...), kind=kOutput, calls=%fused_computation.41 | convolution fusion | flops 555745280 | bytes 16859392 | tf_op jit(solution)/shard_map/nhqk,nkhd->nqhd/dot_general | solution.py:147
  158.6 4.4 %copy.180 = f32[4,128,16,128]{3,2,1,0:T(8,128)} copy(f32[4,128,16,128]{3,1,2,0:T(8,128)S(1)} %fusion.27) | data formatting | bytes 8388608 | tf_op jit(solution)/shard_map/nhqk,nkhd->nqhd/transpose | solution.py:147
  163.1 6.9 %fusion.14 = f32[512,16,128]{2,1,0:T(8,128)S(1)} fusion(f32[4,128,16,128]{3,2,1,0:T(8,128)} %copy.193, f32[4,128,16,128]{3,2,1,0:T(8,128)} %copy.180, f32[512,16]{1,0:T(8,128)S(1)} %copy.182, f32[512,16]{1,0:T(8,128)S(1)} %copy.198), kind=kLoop, calls=%fused_computation.21 | loop fusion | flops 3145728 | bytes 12648448 | tf_op jit(solution)/shard_map/div | solution.py:162
  170.0 14.1 %fusion.23 = f32[512,16]{1,0:T(8,128)S(1)} fusion(f32[512,16,128]{2,1,0:T(8,128)S(1)} %fusion.14, f32[512,16]{1,0:T(8,128)S(1)} %copy.198, bf16[1,512,16,128]{3,2,1,0:T(8,128)(2,1)S(1)} %copy-done.8), kind=kLoop, calls=%fused_computation.33 | loop fusion | flops 4186112 | bytes 6356992 | tf_op jit(solution)/shard_map/reduce_sum | solution.py:164
  186.7 7.5 %fusion.174 = (f32[16,8,128]{2,1,0:T(8,128)S(1)}, f32[4,16,8,128]{3,2,1,0:T(8,128)}) fusion(f32[4,128,16,128]{3,2,1,0:T(8,128)} %convert.3, f32[4,128,16]{1,2,0:T(8,128)S(1)} %get-tuple-element.351, f32[4,128,16]{1,2,0:T(8,128)S(1)} %copy-done.28, f32[512,16,8]{0,2,1:T(8,128)S(1)} %copy-done.14), kind=kOutput, calls=%fused_computation.200 | convolution fusion | flops 103202816 | bytes 4849664 | tf_op jit(solution)/shard_map/nthr,nthd->nhrd/dot_general | solution.py:171
  194.2 31.2 %all-gather.2 = f32[128,8,128]{2,1,0:T(8,128)S(1)} all-gather(f32[16,8,128]{2,1,0:T(8,128)S(1)} %get-tuple-element.358), channel_id=4, replica_groups=mesh['seq'=8,'batch'=4] {'seq'}, dimensions={0}, use_global_device_ids=true | all-gather | bytes 589824 | tf_op jit(solution)/shard_map/all_gather | solution.py:21
  225.4 30.6 %all-gather.5 = f32[8,16,8]{1,2,0:T(8,128)S(1)} all-gather(f32[1,16,8]{1,2,0:T(8,128)S(1)} %bitcast.245), channel_id=5, replica_groups=mesh['seq'=8,'batch'=4] {'seq'}, dimensions={0}, use_global_device_ids=true | all-gather | bytes 4608 | tf_op jit(solution)/shard_map/all_gather | solution.py:21
  262.2 9.5 %fusion.76 = f32[4,128,16,8]{1,3,2,0:T(8,128)S(1)} fusion(f32[4,128,16,128]{3,2,1,0:T(8,128)} %convert.3, f32[4,128,16]{1,2,0:T(8,128)} %copy-done.31, f32[4,128,16]{1,2,0:T(8,128)} %get-tuple-element.352, f32[4,16,8,128]{3,0,2,1:T(4,128)} %copy-done.15, f32[4,16,8]{2,1,0:T(8,128)} %copy.207, f32[4,128,16]{1,2,0:T(8,128)} %copy-done.30), kind=kOutput, calls=%fused_computation.74 | convolution fusion | flops 102891520 | bytes 4818944 | tf_op jit(solution)/shard_map/nthd,nhrd->nthr/dot_general | solution.py:168
  273.7 4.1 fusion.51
  277.9 4.1 fusion.57
  282.1 3.1 fusion.47
  285.1 7.2 %fusion.18 = bf16[1,512,16,128]{3,2,1,0:T(8,128)(2,1)} fusion(f32[512,16]{1,0:T(8,128)S(1)} %copy.198, f32[512,16]{1,0:T(8,128)S(1)} %copy.182, f32[1,512,16,128]{3,2,1,0:T(8,128)} %bitcast.221, f32[1,512,16,128]{3,2,1,0:T(8,128)} %bitcast.222), kind=kLoop, calls=%fused_computation.27 | loop fusion | flops 4194304 | bytes 10551296 | tf_op jit(solution)/shard_map/convert_element_type | solution.py:203
  292.4 117.7 %all-reduce.4.cloned.1.call-done = (f32[16,128,8]{1,2,0:T(8,128)}, f32[16,128,8]{1,2,0:T(8,128)}) async-done(((f32[16,128,8]{1,2,0:T(8,128)}, f32[16,128,8]{1,2,0:T(8,128)}), (f32[16,128,8]{1,2,0:T(8,128)}, f32[16,128,8]{1,2,0:T(8,128)})) %all-reduce.4.cloned.1.call-update) | async-done | bytes 131088 | tf_op jit(solution)/shard_map/psum | solution.py:202
  (194 shorter events, 58.0 us)
Async XLA Ops:
  7.2 26.6 %copy-start = (bf16[1,512,16,128]{3,2,1,0:T(8,128)(2,1)S(1)}, bf16[1,512,16,128]{3,2,1,0:T(8,128)(2,1)}, u32[]{:S(2)}) copy-start(bf16[1,512,16,128]{3,2,1,0:T(8,128)(2,1)} %param.11) | copy-start | bytes 6291460
  7.2 16.6 %copy-start.37 = (s32[1,16,32]{2,1,0:T(8,128)S(1)}, s32[1,16,32]{2,1,0:T(8,128)}, u32[]{:S(2)}) copy-start(s32[1,16,32]{2,1,0:T(8,128)} %param.14) | copy-start | bytes 6148
  7.2 402.9 %all-reduce.4.cloned.1.call-start = ((), (), s32[]{:S(2)}) async-start(), calls=%async_computation | async-start | bytes 262144 | tf_op jit(solution)/shard_map/psum | solution.py:202
  11.7 23.6 %collective-permute-start.1 = (bf16[128,16,128]{2,0,1:T(8,128)(2,1)}, bf16[128,16,128]{2,0,1:T(8,128)(2,1)}, u32[]{:S(2)}, u32[]{:S(2)}) collective-permute-start(bf16[128,16,128]{2,0,1:T(8,128)(2,1)} %slice_bitcast_fusion), channel_id=1, source_target_pairs={{0,4},{4,8},{8,12},{12,16},{16,20},{20,24},{24,28},{1,5},{5,9},{9,... | collective-permute-start | bytes 1572872 | tf_op jit(solution)/shard_map/ppermute | solution.py:16
  19.3 20.4 %collective-permute-start = (bf16[128,16,128]{2,1,0:T(8,128)(2,1)}, bf16[128,16,128]{2,1,0:T(8,128)(2,1)S(1)}, u32[]{:S(2)}, u32[]{:S(2)}) collective-permute-start(bf16[128,16,128]{2,1,0:T(8,128)(2,1)} %slice_bitcast_fusion.1), channel_id=1, source_target_pairs={{0,4},{4,8},{8,12},{12,16},{16,20},{20,24},{24,28},{1,5},{5,9},{9,... | collective-permute-start | bytes 1572872 | tf_op jit(solution)/shard_map/ppermute | solution.py:16
  22.0 15.3 %copy-start.32 = (f32[640]{0:T(1024)}, f32[640]{0:T(1024)S(1)}, u32[]{:S(2)}) copy-start(f32[640]{0:T(1024)S(1)} %fusion.149) | copy-start | bytes 7684
  22.0 114.2 %copy-start.34 = (s32[4]{0:T(128)}, s32[4]{0:T(128)S(1)}, u32[]{:S(2)}) copy-start(s32[4]{0:T(128)S(1)} %iota_add_fusion.1) | copy-start | bytes 52
  111.2 12.2 %copy-start.38 = (f32[5]{0:T(128)S(1)}, f32[5]{0:T(128)}, u32[]{:S(2)}) copy-start(f32[5]{0:T(128)} %broadcast_subtract_fusion) | copy-start | bytes 64
  111.2 12.2 %copy-start.40 = (f32[5]{0:T(128)S(1)}, f32[5]{0:T(128)}, u32[]{:S(2)}) copy-start(f32[5]{0:T(128)} %compare_convert_fusion.1) | copy-start | bytes 64
  118.9 6.0 %copy-start.13 = (f32[512,16,8]{0,2,1:T(8,128)S(1)}, f32[512,16,8]{0,2,1:T(8,128)}, u32[]{:S(2)}) copy-start(f32[512,16,8]{0,2,1:T(8,128)} %fusion.73) | copy-start | bytes 786436
  131.6 5.8 %copy-start.14 = (f32[512,16,8]{0,2,1:T(8,128)S(1)}, f32[512,16,8]{0,2,1:T(8,128)}, u32[]{:S(2)}) copy-start(f32[512,16,8]{0,2,1:T(8,128)} %fusion.73) | copy-start | bytes 786436
  138.2 10.1 %copy-start.23 = (f32[4,16,1,128]{3,2,1,0:T(1,128)}, f32[4,16,1,128]{3,2,1,0:T(1,128)S(1)}, u32[]{:S(2)}) copy-start(f32[4,16,1,128]{3,2,1,0:T(1,128)S(1)} %fusion.112) | copy-start | bytes 98308
  142.8 4.8 %copy-start.9 = (f32[4,16,256,128]{3,2,1,0:T(8,128)}, f32[4,16,256,128]{3,2,1,0:T(8,128)S(1)}, u32[]{:S(2)}) copy-start(f32[4,16,256,128]{3,2,1,0:T(8,128)S(1)} %get-tuple-element.357) | copy-start | bytes 25165828
  163.1 6.9 %copy-start.8 = (bf16[1,512,16,128]{3,2,1,0:T(8,128)(2,1)S(1)}, bf16[1,512,16,128]{3,2,1,0:T(8,128)(2,1)}, u32[]{:S(2)}) copy-start(bf16[1,512,16,128]{3,2,1,0:T(8,128)(2,1)} %param.17) | copy-start | bytes 6291460
  170.0 14.2 %copy-start.24 = (f32[4,16,1,128]{3,2,1,0:T(1,128)S(1)}, f32[4,16,1,128]{3,2,1,0:T(1,128)}, u32[]{:S(2)}) copy-start(f32[4,16,1,128]{3,2,1,0:T(1,128)} %copy-done.23) | copy-start | bytes 98308
  170.0 15.0 %copy-start.35 = (s32[4]{0:T(128)S(1)}, s32[4]{0:T(128)}, u32[]{:S(2)}) copy-start(s32[4]{0:T(128)} %copy-done.34) | copy-start | bytes 52
  170.0 16.6 %copy-start.28 = (f32[4,128,16]{1,2,0:T(8,128)S(1)}, f32[4,128,16]{1,2,0:T(8,128)}, u32[]{:S(2)}) copy-start(f32[4,128,16]{1,2,0:T(8,128)} %get-tuple-element.352) | copy-start | bytes 98308
  184.3 9.9 %copy-start.30 = (f32[4,128,16]{1,2,0:T(8,128)}, f32[4,128,16]{1,2,0:T(8,128)S(1)}, u32[]{:S(2)}) copy-start(f32[4,128,16]{1,2,0:T(8,128)S(1)} %get-tuple-element.350) | copy-start | bytes 98308
  184.3 9.9 %copy-start.31 = (f32[4,128,16]{1,2,0:T(8,128)}, f32[4,128,16]{1,2,0:T(8,128)S(1)}, u32[]{:S(2)}) copy-start(f32[4,128,16]{1,2,0:T(8,128)S(1)} %get-tuple-element.351) | copy-start | bytes 98308
  186.6 69.3 %copy-start.25 = (f32[16,8]{0,1:T(8,128)S(1)}, f32[16,8]{0,1:T(8,128)}, u32[]{:S(2)}) copy-start(f32[16,8]{0,1:T(8,128)} %custom-call.3) | copy-start | bytes 1540
  186.6 70.1 %copy-start.36 = (s32[4]{0:T(128)S(1)}, s32[4]{0:T(128)}, u32[]{:S(2)}) copy-start(s32[4]{0:T(128)} %copy-done.34) | copy-start | bytes 52
  186.6 70.1 %copy-start.39 = (f32[5]{0:T(128)S(1)}, f32[5]{0:T(128)}, u32[]{:S(2)}) copy-start(f32[5]{0:T(128)} %broadcast_subtract_fusion) | copy-start | bytes 64
  186.6 70.1 %copy-start.41 = (f32[5]{0:T(128)S(1)}, f32[5]{0:T(128)}, u32[]{:S(2)}) copy-start(f32[5]{0:T(128)} %compare_convert_fusion.1) | copy-start | bytes 64
  186.6 70.1 %copy-start.43 = (f32[5]{0:T(128)S(1)}, f32[5]{0:T(128)}, u32[]{:S(2)}) copy-start(f32[5]{0:T(128)} %compare_convert_fusion) | copy-start | bytes 64
  (24 other events, 70.9 us)
Sparse Core Ops, SparseCore 0:
  285.3 124.7 all-reduce.3
where the time goes:
time: 427 us; the launch traced here: 420 us
  blocking collectives  128 us (30%)
  waiting for transfers between devices  118 us (28%)
  matrix products  64.9 us (15%)
  other arithmetic  52 us (12%)
  local copies, waits for them, and re-layouts  33.3 us (8%)
  between operations  15.1 us (4%)
  starting transfers between devices  8.39 us (2%)
    all_gather x4, blocking collectives, prefix(): everything = jax.tree.map(lambda part: lax.all_gather(part, axis), shard)  128 us
    psum x1, waiting for transfers between devices, body(): grad_q, grad_k = lax.psum((grad_q, grad_k), ('seq', 'batch'))  118 us
    reduce_sum x1, other arithmetic, body(): ratio_grad = -jnp.sum(delta * out, -1)  14.1 us
    unnamed x93, local copies, waits for them, and re-layouts  11.3 us
    dot_general x1, matrix products, body(): jnp.einsum('nthd,nhrd->nthr', grad_num, state, precision=HIGHEST)  9.54 us
  transfers between devices with their start and end apart: 3, of which 1 were waited for; matrix products, arithmetic and copies ran while one was open for 6% of the time, Pallas kernels for 0%

commit v1 on v0

--- a/solution.py
+++ b/solution.py
@@ -1,3 +1,4 @@
+import functools
 import math
 import jax
 import jax.numpy as jnp
@@ -8,6 +9,15 @@
 WINDOW = 256
 HIGHEST = lax.Precision.HIGHEST
 feature_shift = 1.5
+
+
+def _get_core(raw, comm_axis, device_axis):
+    for to_i in (device_axis, comm_axis):
+        raw = jax.lax.psum(raw, to_i)
+    return raw
+
+
+make_sites = functools.partial(_get_core, comm_axis="seq", device_axis="batch")
 
 
 def passed_along(value, axis, steps):
@@ -199,7 +209,7 @@
     grad_pre_q = grad_fq.reshape(tokens, heads, rank) * jax.nn.sigmoid(pre_q)
     grad_q = jnp.einsum("thd,thr->hdr", q_rows.astype(jnp.float32), grad_pre_q, precision=HIGHEST)
     grad_k = jnp.einsum("thd,thr->hdr", ext_keys.astype(jnp.float32), grad_pre_k, precision=HIGHEST)
-    grad_q, grad_k = lax.psum((grad_q, grad_k), ("seq", "batch"))
+    grad_q, grad_k = make_sites((grad_q, grad_k))
     return (out.astype(jnp.bfloat16)[None], grad_q, grad_k)
 
 

time: 427 us -> 408 us (0.956)
  waiting for transfers between devices: 118 us -> 98.8 us
    psum x1 -> x2, waiting for transfers between devices: 118 us -> 98.7 us  [_get_core(): raw = jax.lax.psum(raw, to_i)]
  transfers between devices with their start and end apart: 3 -> 4, of which waited for: 1 -> 2; matrix products, arithmetic and copies ran while one was open for 6% -> 6% of each run, Pallas kernels for 0% -> 0%
where the time goes in v1:
time: 408 us; the launch traced here: 401 us
  blocking collectives  128 us (31%)
  waiting for transfers between devices  98.8 us (24%)
  matrix products  64.9 us (16%)
  other arithmetic  51.9 us (13%)
  local copies, waits for them, and re-layouts  33.3 us (8%)
  between operations  15.1 us (4%)
  starting transfers between devices  8.43 us (2%)
    all_gather x4, blocking collectives, prefix(): everything = jax.tree.map(lambda part: lax.all_gather(part, axis), shard)  128 us
    psum x2, waiting for transfers between devices, _get_core(): raw = jax.lax.psum(raw, to_i)  98.7 us
    reduce_sum x1, other arithmetic, body(): ratio_grad = -jnp.sum(delta * out, -1)  14.1 us
    unnamed x93, local copies, waits for them, and re-layouts  11.3 us
    dot_general x1, matrix products, body(): jnp.einsum('nthd,nhrd->nthr', grad_num, state, precision=HIGHEST)  9.54 us
    ppermute x2, starting transfers between devices, passed_along(): lax.ppermute(value, axis, [(source, source + steps) for source in range(f...  8.35 us
  transfers between devices with their start and end apart: 4, of which 2 were waited for; matrix products, arithmetic and copies ran while one was open for 6% of the time, Pallas kernels for 0%

profile of v1, /device:TPU:0, one launch (start us, length us, event | category | flops | bytes accessed | tf_op | source)
XLA Modules:
  0.0 401.4 jit_solution(10032189386831203963)
XLA Ops:
  11.7 5.7 %collective-permute-start.1 = (bf16[128,16,128]{2,0,1:T(8,128)(2,1)}, bf16[128,16,128]{2,0,1:T(8,128)(2,1)}, u32[]{:S(2)}, u32[]{:S(2)}) collective-permute-start(bf16[128,16,128]{2,0,1:T(8,128)(2,1)} %slice_bitcast_fusion), channel_id=1, source_target_pairs={{0,4},{4,8},{8,12},{12,16},{16,20},{20,24},{24,28},{1,5},{5,9},{9,... | collective-permute-start | bytes 1572872 | tf_op jit(solution)/shard_map/ppermute | solution.py:26
  25.8 3.5 copy.177
  45.1 35.4 %all-gather = f32[128,8,128]{2,1,0:T(8,128)} all-gather(f32[16,8,128]{2,1,0:T(8,128)S(1)} %slice_reduce_fusion), channel_id=2, replica_groups=mesh['seq'=8,'batch'=4] {'seq'}, dimensions={0}, use_global_device_ids=true | all-gather | bytes 589824 | tf_op jit(solution)/shard_map/all_gather | solution.py:31
  80.6 30.6 %all-gather.4 = f32[8,16,8]{1,2,0:T(8,128)S(1)} all-gather(f32[1,16,8]{1,2,0:T(8,128)S(1)} %bitcast.246), channel_id=3, replica_groups=mesh['seq'=8,'batch'=4] {'seq'}, dimensions={0}, use_global_device_ids=true | all-gather | bytes 4608 | tf_op jit(solution)/shard_map/all_gather | solution.py:31
  111.2 7.7 %while.34 = (s32[]{:T(128)}, f32[16,8,128]{2,1,0:T(8,128)S(1)}, f32[16,8]{0,1:T(8,128)S(1)}, s32[]{:T(128)}, f32[8,16,8,128]{3,2,1,0:T(8,128)}, /*index=5*/f32[8,16,8]{1,2,0:T(8,128)S(1)}, s32[]{:T(128)}, s32[]{:T(128)}) while((s32[]{:T(128)}, f32[16,8,128]{2,1,0:T(8,128)S(1)}, f32[16,8]{0,1:T(8,128)S(1)}, s32[]{:T(128)}, ...), condition=%wide.region_5.6_spmd.clone, body=%wide.region_4.5_spmd.clone.sunk | while | flops 49540 | bytes 198259 | solution.py:44
  118.9 3.9 fusion.42
  124.9 6.7 %convolution_bitcast_fusion = f32[4,128,16,128]{3,1,2,0:T(8,128)S(1)} fusion(f32[4,16,8,128]{3,0,2,1:T(4,128)S(1)} %fusion.66, f32[512,16,8]{0,2,1:T(8,128)S(1)} %copy-done.13), kind=kOutput, calls=%fused_computation.42 | convolution fusion | flops 101056512 | bytes 4718592 | tf_op jit(solution)/shard_map/nthr,nhrd->nthd/dot_general | solution.py:165
  131.6 4.5 %copy.193 = f32[4,128,16,128]{3,2,1,0:T(8,128)} copy(f32[4,128,16,128]{3,1,2,0:T(8,128)S(1)} %convolution_bitcast_fusion) | data formatting | bytes 8388608 | tf_op jit(solution)/shard_map/nthr,nhrd->nthd/transpose | solution.py:165
  139.9 2.9 fusion
  143.5 4.1 %fusion.2 = f32[4,16,128]{2,1,0:T(8,128)S(1)} fusion(f32[4,16,256,128]{3,2,1,0:T(8,128)S(1)} %get-tuple-element.359, f32[4,16,128]{2,1,0:T(8,128)S(1)} %get-tuple-element.358, pred[4,16,256]{2,1,0:T(8,128)(4,1)S(1)} %copy-done.26, pred[128,256]{0,1:T(8,128)(4,1)S(1)} %copy-done.21, pred[256]{0:T(512)(128)(4,1)S(1)} %copy-done.42), kind=kLoop, calls=%fused_computation.9 | loop fusion | flops 10477568 | bytes 8503552 | tf_op jit(solution)/shard_map/reduce_sum | solution.py:156
  152.3 6.3 %fusion.27 = f32[4,128,16,128]{3,1,2,0:T(8,128)S(1)} fusion(f32[4,16,256,128]{3,2,1,0:T(8,128)S(1)} %copy-done.10, f32[4,16,128]{2,1,0:T(8,128)S(1)} %get-tuple-element.358, pred[4,16,256]{2,1,0:T(8,128)(4,1)S(1)} %copy-done.26, pred[128,256]{0,1:T(8,128)(4,1)S(1)} %copy-done.21, pred[256]{0:T(512)(128)(4,1)S(1)} %copy-done.42, ...), kind=kOutput, calls=%fused_computation.41 | convolution fusion | flops 555745280 | bytes 16859392 | tf_op jit(solution)/shard_map/nhqk,nkhd->nqhd/dot_general | solution.py:157
  158.6 4.4 %copy.180 = f32[4,128,16,128]{3,2,1,0:T(8,128)} copy(f32[4,128,16,128]{3,1,2,0:T(8,128)S(1)} %fusion.27) | data formatting | bytes 8388608 | tf_op jit(solution)/shard_map/nhqk,nkhd->nqhd/transpose | solution.py:157
  163.1 6.9 %fusion.14 = f32[512,16,128]{2,1,0:T(8,128)S(1)} fusion(f32[4,128,16,128]{3,2,1,0:T(8,128)} %copy.193, f32[4,128,16,128]{3,2,1,0:T(8,128)} %copy.180, f32[512,16]{1,0:T(8,128)S(1)} %copy.182, f32[512,16]{1,0:T(8,128)S(1)} %copy.198), kind=kLoop, calls=%fused_computation.21 | loop fusion | flops 3145728 | bytes 12648448 | tf_op jit(solution)/shard_map/div | solution.py:172
  170.0 14.1 %fusion.23 = f32[512,16]{1,0:T(8,128)S(1)} fusion(f32[512,16,128]{2,1,0:T(8,128)S(1)} %fusion.14, f32[512,16]{1,0:T(8,128)S(1)} %copy.198, bf16[1,512,16,128]{3,2,1,0:T(8,128)(2,1)S(1)} %copy-done.8), kind=kLoop, calls=%fused_computation.33 | loop fusion | flops 4186112 | bytes 6356992 | tf_op jit(solution)/shard_map/reduce_sum | solution.py:174
  186.7 7.5 %fusion.174 = (f32[16,8,128]{2,1,0:T(8,128)S(1)}, f32[4,16,8,128]{3,2,1,0:T(8,128)}) fusion(f32[4,128,16,128]{3,2,1,0:T(8,128)} %convert.3, f32[4,128,16]{1,2,0:T(8,128)S(1)} %get-tuple-element.353, f32[4,128,16]{1,2,0:T(8,128)S(1)} %copy-done.28, f32[512,16,8]{0,2,1:T(8,128)S(1)} %copy-done.14), kind=kOutput, calls=%fused_computation.200 | convolution fusion | flops 103202816 | bytes 4849664 | tf_op jit(solution)/shard_map/nthr,nthd->nhrd/dot_general | solution.py:181
  194.2 31.2 %all-gather.2 = f32[128,8,128]{2,1,0:T(8,128)S(1)} all-gather(f32[16,8,128]{2,1,0:T(8,128)S(1)} %get-tuple-element.360), channel_id=4, replica_groups=mesh['seq'=8,'batch'=4] {'seq'}, dimensions={0}, use_global_device_ids=true | all-gather | bytes 589824 | tf_op jit(solution)/shard_map/all_gather | solution.py:31
  225.4 30.6 %all-gather.5 = f32[8,16,8]{1,2,0:T(8,128)S(1)} all-gather(f32[1,16,8]{1,2,0:T(8,128)S(1)} %bitcast.245), channel_id=5, replica_groups=mesh['seq'=8,'batch'=4] {'seq'}, dimensions={0}, use_global_device_ids=true | all-gather | bytes 4608 | tf_op jit(solution)/shard_map/all_gather | solution.py:31
  262.2 9.5 %fusion.76 = f32[4,128,16,8]{1,3,2,0:T(8,128)S(1)} fusion(f32[4,128,16,128]{3,2,1,0:T(8,128)} %convert.3, f32[4,128,16]{1,2,0:T(8,128)} %copy-done.31, f32[4,128,16]{1,2,0:T(8,128)} %get-tuple-element.354, f32[4,16,8,128]{3,0,2,1:T(4,128)} %copy-done.15, f32[4,16,8]{2,1,0:T(8,128)} %copy.207, f32[4,128,16]{1,2,0:T(8,128)} %copy-done.30), kind=kOutput, calls=%fused_computation.74 | convolution fusion | flops 102891520 | bytes 4818944 | tf_op jit(solution)/shard_map/nthd,nhrd->nthr/dot_general | solution.py:178
  273.7 4.1 %fusion.51 = f32[5,128,16,8]{1,3,2,0:T(8,128)S(1)} fusion(bf16[5,128,16,128]{3,2,1,0:T(8,128)(2,1)S(1)} %bitcast.225, f32[5,16,8,128]{3,0,2,1:T(8,128)S(1)} %copy-done.16, f32[5,16,8]{2,1,0:T(8,128)S(1)} %copy.214), kind=kOutput, calls=%fused_computation.62 | convolution fusion | flops 125911040 | bytes 3279360 | tf_op jit(solution)/shard_map/nhrd,nthd->nthr/dot_general | solution.py:203
  277.9 4.1 %fusion.57 = f32[5,128,16,8]{1,3,2,0:T(8,128)S(1)} fusion(bf16[5,128,16,128]{3,2,1,0:T(8,128)(2,1)S(1)} %bitcast.226, f32[5,16,8,128]{3,0,2,1:T(8,128)S(1)} %fusion.106, f32[5,16,8]{2,1,0:T(8,128)S(1)} %copy.219), kind=kOutput, calls=%fused_computation.64 | convolution fusion | flops 125911040 | bytes 3279360 | tf_op jit(solution)/shard_map/nhrd,nthd->nthr/dot_general | solution.py:204
  282.1 3.1 fusion.47
  285.2 31.8 %all-reduce.8.cloned.1.call-done = (f32[16,128,8]{1,2,0:T(8,128)}, f32[16,128,8]{1,2,0:T(8,128)}) async-done(((f32[16,128,8]{1,2,0:T(8,128)}, f32[16,128,8]{1,2,0:T(8,128)}), (f32[16,128,8]{1,2,0:T(8,128)}, f32[16,128,8]{1,2,0:T(8,128)})) %all-reduce.8.cloned.1.call-update) | async-done | bytes 131088 | tf_op jit(solution)/shard_map/psum | solution.py:16
  317.0 7.2 %fusion.18 = bf16[1,512,16,128]{3,2,1,0:T(8,128)(2,1)} fusion(f32[512,16]{1,0:T(8,128)S(1)} %copy.198, f32[512,16]{1,0:T(8,128)S(1)} %copy.182, f32[1,512,16,128]{3,2,1,0:T(8,128)} %bitcast.221, f32[1,512,16,128]{3,2,1,0:T(8,128)} %bitcast.222), kind=kLoop, calls=%fused_computation.27 | loop fusion | flops 4194304 | bytes 10551296 | tf_op jit(solution)/shard_map/convert_element_type | solution.py:213
  324.3 66.9 %all-reduce.6.cloned.1.call-done = (f32[16,128,8]{1,2,0:T(8,128)}, f32[16,128,8]{1,2,0:T(8,128)}) async-done(((f32[16,128,8]{1,2,0:T(8,128)}, f32[16,128,8]{1,2,0:T(8,128)}), (f32[16,128,8]{1,2,0:T(8,128)}, f32[16,128,8]{1,2,0:T(8,128)})) %all-reduce.6.cloned.1.call-update) | async-done | bytes 131088 | tf_op jit(solution)/shard_map/psum | solution.py:16
  (197 shorter events, 60.6 us)
Async XLA Ops:
  7.2 26.5 %copy-start = (bf16[1,512,16,128]{3,2,1,0:T(8,128)(2,1)S(1)}, bf16[1,512,16,128]{3,2,1,0:T(8,128)(2,1)}, u32[]{:S(2)}) copy-start(bf16[1,512,16,128]{3,2,1,0:T(8,128)(2,1)} %param.11) | copy-start | bytes 6291460
  7.2 16.6 %copy-start.37 = (s32[1,16,32]{2,1,0:T(8,128)S(1)}, s32[1,16,32]{2,1,0:T(8,128)}, u32[]{:S(2)}) copy-start(s32[1,16,32]{2,1,0:T(8,128)} %param.14) | copy-start | bytes 6148
  7.2 309.8 %all-reduce.8.cloned.1.call-start = ((), (), s32[]{:S(2)}) async-start(), calls=%async_computation.1 | async-start | bytes 262144 | tf_op jit(solution)/shard_map/psum | solution.py:16
  11.7 23.5 %collective-permute-start.1 = (bf16[128,16,128]{2,0,1:T(8,128)(2,1)}, bf16[128,16,128]{2,0,1:T(8,128)(2,1)}, u32[]{:S(2)}, u32[]{:S(2)}) collective-permute-start(bf16[128,16,128]{2,0,1:T(8,128)(2,1)} %slice_bitcast_fusion), channel_id=1, source_target_pairs={{0,4},{4,8},{8,12},{12,16},{16,20},{20,24},{24,28},{1,5},{5,9},{9,... | collective-permute-start | bytes 1572872 | tf_op jit(solution)/shard_map/ppermute | solution.py:26
  19.3 20.3 %collective-permute-start = (bf16[128,16,128]{2,1,0:T(8,128)(2,1)}, bf16[128,16,128]{2,1,0:T(8,128)(2,1)S(1)}, u32[]{:S(2)}, u32[]{:S(2)}) collective-permute-start(bf16[128,16,128]{2,1,0:T(8,128)(2,1)} %slice_bitcast_fusion.1), channel_id=1, source_target_pairs={{0,4},{4,8},{8,12},{12,16},{16,20},{20,24},{24,28},{1,5},{5,9},{9,... | collective-permute-start | bytes 1572872 | tf_op jit(solution)/shard_map/ppermute | solution.py:26
  22.0 15.2 %copy-start.32 = (f32[640]{0:T(1024)}, f32[640]{0:T(1024)S(1)}, u32[]{:S(2)}) copy-start(f32[640]{0:T(1024)S(1)} %fusion.149) | copy-start | bytes 7684
  22.0 114.2 %copy-start.34 = (s32[4]{0:T(128)}, s32[4]{0:T(128)S(1)}, u32[]{:S(2)}) copy-start(s32[4]{0:T(128)S(1)} %iota_add_fusion.1) | copy-start | bytes 52
  111.2 12.2 %copy-start.38 = (f32[5]{0:T(128)S(1)}, f32[5]{0:T(128)}, u32[]{:S(2)}) copy-start(f32[5]{0:T(128)} %broadcast_subtract_fusion) | copy-start | bytes 64
  111.2 12.2 %copy-start.40 = (f32[5]{0:T(128)S(1)}, f32[5]{0:T(128)}, u32[]{:S(2)}) copy-start(f32[5]{0:T(128)} %compare_convert_fusion.1) | copy-start | bytes 64
  118.8 6.0 %copy-start.13 = (f32[512,16,8]{0,2,1:T(8,128)S(1)}, f32[512,16,8]{0,2,1:T(8,128)}, u32[]{:S(2)}) copy-start(f32[512,16,8]{0,2,1:T(8,128)} %fusion.73) | copy-start | bytes 786436
  131.6 5.9 %copy-start.14 = (f32[512,16,8]{0,2,1:T(8,128)S(1)}, f32[512,16,8]{0,2,1:T(8,128)}, u32[]{:S(2)}) copy-start(f32[512,16,8]{0,2,1:T(8,128)} %fusion.73) | copy-start | bytes 786436
  138.2 10.1 %copy-start.23 = (f32[4,16,1,128]{3,2,1,0:T(1,128)}, f32[4,16,1,128]{3,2,1,0:T(1,128)S(1)}, u32[]{:S(2)}) copy-start(f32[4,16,1,128]{3,2,1,0:T(1,128)S(1)} %fusion.112) | copy-start | bytes 98308
  163.1 6.9 %copy-start.8 = (bf16[1,512,16,128]{3,2,1,0:T(8,128)(2,1)S(1)}, bf16[1,512,16,128]{3,2,1,0:T(8,128)(2,1)}, u32[]{:S(2)}) copy-start(bf16[1,512,16,128]{3,2,1,0:T(8,128)(2,1)} %param.17) | copy-start | bytes 6291460
  170.0 14.2 %copy-start.24 = (f32[4,16,1,128]{3,2,1,0:T(1,128)S(1)}, f32[4,16,1,128]{3,2,1,0:T(1,128)}, u32[]{:S(2)}) copy-start(f32[4,16,1,128]{3,2,1,0:T(1,128)} %copy-done.23) | copy-start | bytes 98308
  170.0 15.0 %copy-start.35 = (s32[4]{0:T(128)S(1)}, s32[4]{0:T(128)}, u32[]{:S(2)}) copy-start(s32[4]{0:T(128)} %copy-done.34) | copy-start | bytes 52
  170.0 16.6 %copy-start.28 = (f32[4,128,16]{1,2,0:T(8,128)S(1)}, f32[4,128,16]{1,2,0:T(8,128)}, u32[]{:S(2)}) copy-start(f32[4,128,16]{1,2,0:T(8,128)} %get-tuple-element.354) | copy-start | bytes 98308
  184.2 9.9 %copy-start.30 = (f32[4,128,16]{1,2,0:T(8,128)}, f32[4,128,16]{1,2,0:T(8,128)S(1)}, u32[]{:S(2)}) copy-start(f32[4,128,16]{1,2,0:T(8,128)S(1)} %get-tuple-element.352) | copy-start | bytes 98308
  184.3 9.9 %copy-start.31 = (f32[4,128,16]{1,2,0:T(8,128)}, f32[4,128,16]{1,2,0:T(8,128)S(1)}, u32[]{:S(2)}) copy-start(f32[4,128,16]{1,2,0:T(8,128)S(1)} %get-tuple-element.353) | copy-start | bytes 98308
  186.6 69.3 %copy-start.25 = (f32[16,8]{0,1:T(8,128)S(1)}, f32[16,8]{0,1:T(8,128)}, u32[]{:S(2)}) copy-start(f32[16,8]{0,1:T(8,128)} %custom-call.3) | copy-start | bytes 1540
  186.6 70.1 %copy-start.36 = (s32[4]{0:T(128)S(1)}, s32[4]{0:T(128)}, u32[]{:S(2)}) copy-start(s32[4]{0:T(128)} %copy-done.34) | copy-start | bytes 52
  186.6 70.1 %copy-start.39 = (f32[5]{0:T(128)S(1)}, f32[5]{0:T(128)}, u32[]{:S(2)}) copy-start(f32[5]{0:T(128)} %broadcast_subtract_fusion) | copy-start | bytes 64
  186.6 70.1 %copy-start.41 = (f32[5]{0:T(128)S(1)}, f32[5]{0:T(128)}, u32[]{:S(2)}) copy-start(f32[5]{0:T(128)} %compare_convert_fusion.1) | copy-start | bytes 64
  186.6 70.1 %copy-start.43 = (f32[5]{0:T(128)S(1)}, f32[5]{0:T(128)}, u32[]{:S(2)}) copy-start(f32[5]{0:T(128)} %compare_convert_fusion) | copy-start | bytes 64
  285.2 106.0 %all-reduce.6.cloned.1.call-start = ((), (), s32[]{:S(2)}) async-start(), calls=%async_computation | async-start | bytes 262144 | tf_op jit(solution)/shard_map/psum | solution.py:16
  (25 other events, 75.7 us)
Sparse Core Ops, SparseCore 0:
  285.3 31.6 all-reduce.7
  320.5 70.6 all-reduce.5
